TPU v7x, 32 devices: a whole 2x2x4 slice. The times are simulated.
32 devices in a mesh: dp: 2 (over x), tp: 16 (over z, y, core).
Axes of the slice: x: 2, y: 2, z: 4, core: 2. Of those that a mesh axis runs over, the one named last changes fastest.
Arguments:
- x_in: bfloat16 [1024, 7168], P('dp'), parts along dimension 0
- pos_ids: int32 [1024], P('dp'), parts along dimension 0
- ckv_cache: bfloat16 [2, 1024, 256, 512], P(None, 'dp'), parts along dimension 1
- kpe_cache: bfloat16 [2, 1024, 256, 64], P(None, 'dp'), parts along dimension 1
- attn_gain: bfloat16 [2, 7168], replicated
- w_dq: bfloat16 [2, 7168, 1536], replicated
- q_gain: bfloat16 [2, 1536], replicated
- w_dkv: bfloat16 [2, 7168, 576], replicated
- kv_gain: bfloat16 [2, 512], replicated
- w_uq: bfloat16 [2, 1536, 64, 192], P(None, None, 'tp')
- w_uk: bfloat16 [2, 512, 64, 128], P(None, None, 'tp')
- w_uv: bfloat16 [2, 512, 64, 128], P(None, None, 'tp')
- w_o: bfloat16 [2, 64, 128, 7168], P(None, 'tp')
- mlp_gain: bfloat16 [2, 7168], replicated
- w_gate: bfloat16 [2, 7168, 4608], P(None, None, 'tp')
- w_up: bfloat16 [2, 7168, 4608], P(None, None, 'tp')
- w_down: bfloat16 [2, 4608, 7168], P(None, 'tp')
Outputs:
- output 1: bfloat16 [1024, 7168], P('dp'), parts along dimension 0
- output 2: bfloat16 [2, 1024, 512], P(None, 'dp'), parts along dimension 1
- output 3: bfloat16 [2, 1024, 64], P(None, 'dp'), parts along dimension 1
There are 2 independent parts. A program takes and returns all parts, laid end to end along the dimension named above; an argument that names none is the same for every part.
All inputs are finite; a program needn't handle non-finite values.
Results may differ from a plain program's by a relative error of at most 0.02.
Values are sent between devices in bfloat16 or wider.
A program may use at most 1.75 GiB of HBM per device.

v0:
```python
import math
import jax
import jax.numpy as jnp
from jax import lax
from jax.sharding import PartitionSpec as P

NORM_EPS = 1e-6
ROPE_BASE = 10000.0


def rms_norm(values, norm_gain):
    values = values.astype(jnp.float32)
    inv_rms = lax.rsqrt(jnp.mean(values * values, axis=-1, keepdims=True) + NORM_EPS)
    return (values * inv_rms * norm_gain.astype(jnp.float32)).astype(jnp.bfloat16)


def rotary(values, positions):
    half_dim = values.shape[-1] // 2
    inv_freq = jnp.exp(jnp.arange(half_dim, dtype=jnp.float32) * (-2.0 * math.log(ROPE_BASE) / values.shape[-1]))
    angles = positions.astype(jnp.float32)[..., None] * inv_freq
    cos_part = jnp.cos(angles)
    sin_part = jnp.sin(angles)
    lo_half = values[..., :half_dim]
    hi_half = values[..., half_dim:]
    return jnp.concatenate([lo_half * cos_part - hi_half * sin_part, hi_half * cos_part + lo_half * sin_part], axis=-1)


def latent_attention(q_lat, q_rope, ckv_old, kpe_old, ckv_new, kpe_new, positions, score_scale):
    scores = jnp.einsum('bhc,btc->bht', q_lat, ckv_old, preferred_element_type=jnp.float32)
    scores = scores + jnp.einsum('bhr,btr->bht', q_rope, kpe_old, preferred_element_type=jnp.float32)
    fresh_score = jnp.einsum('bhc,bc->bh', q_lat, ckv_new, preferred_element_type=jnp.float32)
    fresh_score = fresh_score + jnp.einsum('bhr,br->bh', q_rope, kpe_new, preferred_element_type=jnp.float32)
    key_steps = jnp.arange(ckv_old.shape[1])[None, None, :]
    pos_limit = positions[:, None, None]
    at_pos = key_steps == pos_limit
    scores = jnp.where(at_pos, fresh_score[:, :, None], scores) * score_scale
    scores = jnp.where(key_steps <= pos_limit, scores, -jnp.inf)
    attn_prob = jax.nn.softmax(scores, axis=-1).astype(jnp.bfloat16)
    bf_zero = jnp.zeros((), jnp.bfloat16)
    new_prob = jnp.sum(jnp.where(at_pos, attn_prob, bf_zero), axis=-1).astype(jnp.float32)
    context = jnp.einsum('bht,btc->bhc', jnp.where(at_pos, bf_zero, attn_prob), ckv_old, preferred_element_type=jnp.float32)
    context = context + new_prob[:, :, None] * ckv_new.astype(jnp.float32)[:, None, :]
    return context.astype(jnp.bfloat16)


def attention_heads(normed, positions, ckv_old, kpe_old, w_dq, q_gain, w_dkv, kv_gain, w_uq, w_uk, w_uv):
    value_a8 = ckv_old.shape[-1]
    nope_dim = w_uk.shape[-1]
    c_q = rms_norm(jnp.dot(normed, w_dq, preferred_element_type=jnp.float32), q_gain)
    q_full = jnp.einsum('bc,chd->bhd', c_q, w_uq, preferred_element_type=jnp.float32)
    q_nope = q_full[..., :nope_dim].astype(jnp.bfloat16)
    q_rope = rotary(q_full[..., nope_dim:], positions[:, None]).astype(jnp.bfloat16)
    q_lat = jnp.einsum('bhn,chn->bhc', q_nope, w_uk, preferred_element_type=jnp.float32).astype(jnp.bfloat16)
    kv_lat = jnp.dot(normed, w_dkv, preferred_element_type=jnp.float32)
    ckv_new = rms_norm(kv_lat[:, :value_a8], kv_gain)
    kpe_new = rotary(kv_lat[:, value_a8:], positions).astype(jnp.bfloat16)
    context = latent_attention(q_lat, q_rope, ckv_old, kpe_old, ckv_new, kpe_new, positions, w_uq.shape[-1] ** -0.5)
    head_out = jnp.einsum('bhc,chv->bhv', context, w_uv, preferred_element_type=jnp.float32).astype(jnp.bfloat16)
    return head_out, ckv_new, kpe_new


def gated_mlp(mlp_in, w_gate, w_up, w_down):
    gate_pre = jnp.dot(mlp_in, w_gate, preferred_element_type=jnp.float32)
    up_pre = jnp.dot(mlp_in, w_up, preferred_element_type=jnp.float32)
    act_out = (jax.nn.silu(gate_pre) * up_pre).astype(jnp.bfloat16)
    return jnp.dot(act_out, w_down, preferred_element_type=jnp.float32)


def local_layer(hidden, positions, ckv_old, kpe_old, weights):
    (attn_gain, w_dq, q_gain, w_dkv, kv_gain, w_uq, w_uk, w_uv, w_o, mlp_gain, w_gate, w_up, w_down) = weights
    normed = rms_norm(hidden, attn_gain)
    head_out, ckv_new, kpe_new = attention_heads(normed, positions, ckv_old, kpe_old, w_dq, q_gain, w_dkv, kv_gain, w_uq, w_uk, w_uv)
    attn_part = jnp.einsum('bhv,hvd->bd', head_out, w_o, preferred_element_type=jnp.float32).astype(jnp.bfloat16)
    attn_sum = lax.psum(attn_part, 'tp')
    mid_state = (hidden.astype(jnp.float32) + attn_sum.astype(jnp.float32)).astype(jnp.bfloat16)
    mlp_part = gated_mlp(rms_norm(mid_state, mlp_gain), w_gate, w_up, w_down).astype(jnp.bfloat16)
    mlp_sum = lax.psum(mlp_part, 'tp')
    layer_out = (mid_state.astype(jnp.float32) + mlp_sum.astype(jnp.float32)).astype(jnp.bfloat16)
    return layer_out, ckv_new, kpe_new


def solution(mesh):
    cache_spec = P(None, 'dp', None, None)
    head_spec = P(None, None, 'tp', None)
    weight_specs = (P(), P(), P(), P(), P(), head_spec, head_spec, head_spec, P(None, 'tp', None, None), P(), P(None, None, 'tp'), P(None, None, 'tp'), P(None, 'tp', None))
    in_specs = (P('dp', None), P('dp'), cache_spec, cache_spec) + weight_specs
    out_specs = (P('dp', None), P(None, 'dp', None), P(None, 'dp', None))

    def device_body(x_in, pos_ids, ckv_cache, kpe_cache, *params):
        hidden = x_in
        c_rows = []
        k_rows = []
        for layer_idx in range(ckv_cache.shape[0]):
            weights = [weight[layer_idx] for weight in params]
            hidden, c_row, k_row = local_layer(hidden, pos_ids, ckv_cache[layer_idx], kpe_cache[layer_idx], weights)
            c_rows.append(c_row)
            k_rows.append(k_row)
        return hidden, jnp.stack(c_rows), jnp.stack(k_rows)

    return jax.shard_map(device_body, mesh=mesh, in_specs=in_specs, out_specs=out_specs, check_vma=False)
```

profile of v0, /device:TPU:0, one launch (start us, length us, event | category | flops | bytes accessed | tf_op | source)
XLA Modules:
  0.0 1066.9 jit_solution(1811752336110117492)
XLA Ops:
  9.8 4.6 fusion.26
  15.7 7.3 fusion.44
  31.3 19.6 %multiply_reduce_fusion.1 = (f32[512]{0:T(512)S(1)}, f32[512,1536]{1,0:T(8,128)}) fusion(bf16[2,7168,1536]{2,1,0:T(8,128)(2,1)} %param.22, bf16[512,7168]{1,0:T(8,128)(2,1)} %param.17, f32[7168]{0:T(1024)} %bitcast.179, f32[512]{0:T(512)S(1)} %add_rsqrt_fusion.7), kind=kOutput, calls=%fused_computation.89 | convolution fusion | flops 11290542080 | bytes 32538624 | tf_op jit(solution)/shard_map/dot_general | solution.py:49
  58.4 8.2 fusion.22
  66.6 2.5 fusion.91
  69.2 51.6 %multiply_select_fusion.1 = f32[512,4,256]{2,1,0:T(4,128)} fusion(f32[512,4,256]{2,1,0:T(4,128)S(1)} %fusion.22, bf16[2,512,256,512]{3,2,1,0:T(8,128)(2,1)} %param.19, bf16[512,4,512]{2,0,1:T(8,128)(2,1)} %convert_bitcast_fusion.1, f32[512,4]{1,0:T(8,128)S(1)} %add.126, pred[512,256]{1,0:T(8,128)(4,1)S(1)} %copy-done.34, ...), kind=kOutput, calls=%fused_computation.98 | convolution fusion | flops 538968064 | bytes 140779520 | tf_op jit(solution)/shard_map/bhc,btc->bht/dot_general | solution.py:29
  120.8 3.8 fusion.173
  124.6 12.7 %select_reduce_fusion.1 = (bf16[512,4]{1,0:T(8,128)(2,1)S(1)}, bf16[512,4,256]{2,1,0:T(4,128)(2,1)S(1)}) fusion(pred[512,256]{1,0:T(8,128)(4,1)S(1)} %get-tuple-element.41, f32[512,4,256]{2,1,0:T(4,128)S(1)} %get-tuple-element.45, f32[512,4]{1,0:T(8,128)S(1)} %get-tuple-element.44), kind=kLoop, calls=%fused_computation.129 | loop fusion | flops 2095104 | bytes 3289088 | tf_op jit(solution)/shard_map/reduce_sum | solution.py:40
  137.4 43.5 %add_convert_fusion.1 = bf16[512,4,512]{2,1,0:T(4,128)(2,1)} fusion(f32[512,512]{1,0:T(8,128)S(1)} %copy-done.12, f32[512,4]{1,0:T(8,128)S(1)} %convert_element_type.193, bf16[2,512,256,512]{3,2,1,0:T(8,128)(2,1)} %param.19, bf16[512,4,256]{2,1,0:T(4,128)(2,1)S(1)} %get-tuple-element.17, pred[512,256]{1,0:T(8,128)(4,1)S(1)} %get-tuple-element.41), kind=kOutput, calls=%fused_computation.69 | convolution fusion | flops 540540928 | bytes 138551296 | tf_op jit(solution)/shard_map/bht,btc->bhc/dot_general | solution.py:41
  180.9 9.8 bitcast_convert_fusion.1
  192.1 156.4 %all-reduce.5.cloned.1.call-done = bf16[512,7168]{1,0:T(8,128)(2,1)} async-done(((bf16[512,7168]{1,0:T(8,128)(2,1)}), bf16[512,7168]{1,0:T(8,128)(2,1)}) %all-reduce.5.cloned.1.call-update) | async-done | bytes 7340048 | tf_op jit(solution)/shard_map/psum | solution.py:74
  348.5 11.7 %fusion.30 = (f32[512]{0:T(512)S(1)}, bf16[512,7168]{1,0:T(8,128)(2,1)}) fusion(bf16[512,7168]{1,0:T(8,128)(2,1)} %all-reduce.5.cloned.1.call-done, bf16[512,7168]{1,0:T(8,128)(2,1)} %param.17), kind=kLoop, calls=%fused_computation.42 | loop fusion | flops 25689600 | bytes 22022144 | tf_op jit(solution)/shard_map/reduce_sum | solution.py:13
  360.2 6.8 fusion.60
  367.1 4.8 fusion.131
  371.9 6.1 convolution_convert_fusion.1
  378.5 154.5 %all-reduce.7.cloned.1.call-done = bf16[512,7168]{1,0:T(8,128)(2,1)} async-done(((bf16[512,7168]{1,0:T(8,128)(2,1)}), bf16[512,7168]{1,0:T(8,128)(2,1)}) %all-reduce.7.cloned.1.call-update) | async-done | bytes 7340048 | tf_op jit(solution)/shard_map/psum | solution.py:77
  533.0 11.7 %fusion.34 = (f32[512]{0:T(512)S(1)}, bf16[512,7168]{1,0:T(8,128)(2,1)}) fusion(bf16[512,7168]{1,0:T(8,128)(2,1)} %all-reduce.7.cloned.1.call-done, bf16[512,7168]{1,0:T(8,128)(2,1)} %get-tuple-element.15), kind=kLoop, calls=%fused_computation.46 | loop fusion | flops 25689600 | bytes 22022144 | tf_op jit(solution)/shard_map/reduce_sum | solution.py:13
  544.7 9.5 fusion.42
  555.5 19.5 %multiply_reduce_fusion = (f32[512]{0:T(512)S(1)}, f32[512,1536]{1,0:T(8,128)}) fusion(bf16[2,7168,1536]{2,1,0:T(8,128)(2,1)} %param.22, bf16[512,7168]{1,0:T(8,128)(2,1)} %get-tuple-element.13, f32[7168]{0:T(1024)S(1)} %bitcast.175, f32[512]{0:T(512)S(1)} %add_rsqrt_fusion.3), kind=kOutput, calls=%fused_computation.87 | convolution fusion | flops 11290542080 | bytes 32538624 | tf_op jit(solution)/shard_map/dot_general | solution.py:49
  580.7 3.4 fusion.99
  586.8 8.2 fusion.20
  598.2 51.7 %multiply_select_fusion = f32[512,4,256]{2,1,0:T(4,128)} fusion(f32[512,4,256]{2,1,0:T(4,128)S(1)} %fusion.20, bf16[2,512,256,512]{3,2,1,0:T(8,128)(2,1)} %param.19, bf16[512,4,512]{2,0,1:T(8,128)(2,1)} %convert_bitcast_fusion, f32[512,4]{1,0:T(8,128)S(1)} %add.138, pred[512,256]{1,0:T(8,128)(4,1)S(1)} %copy-done.35, pred[512,256]{1,0:T(8,128)(4,1)S(1)} %get-tuple-element.41), kind=kOutput, calls=%fused_computation.95 | convolution fusion | flops 538968064 | bytes 140779520 | tf_op jit(solution)/shard_map/bhc,btc->bht/dot_general | solution.py:29
  649.9 3.8 fusion.174
  655.8 43.5 %add_convert_fusion = bf16[512,4,512]{2,1,0:T(4,128)(2,1)} fusion(f32[512,512]{1,0:T(8,128)S(1)} %copy-done.13, f32[512,4]{1,0:T(8,128)S(1)} %convert_element_type.214, bf16[2,512,256,512]{3,2,1,0:T(8,128)(2,1)} %param.19, bf16[512,4,256]{2,1,0:T(4,128)(2,1)S(1)} %get-tuple-element.11, pred[512,256]{1,0:T(8,128)(4,1)S(1)} %get-tuple-element.41), kind=kOutput, calls=%fused_computation.68 | convolution fusion | flops 540540928 | bytes 138551296 | tf_op jit(solution)/shard_map/bht,btc->bhc/dot_general | solution.py:41
  699.3 9.8 bitcast_convert_fusion
  709.3 155.0 %all-reduce.9.cloned.1.call-done = bf16[512,7168]{1,0:T(8,128)(2,1)} async-done(((bf16[512,7168]{1,0:T(8,128)(2,1)}), bf16[512,7168]{1,0:T(8,128)(2,1)}) %all-reduce.9.cloned.1.call-update) | async-done | bytes 7340048 | tf_op jit(solution)/shard_map/psum | solution.py:74
  864.2 11.7 %fusion.38 = (f32[512]{0:T(512)S(1)}, bf16[512,7168]{1,0:T(8,128)(2,1)}) fusion(bf16[512,7168]{1,0:T(8,128)(2,1)} %all-reduce.9.cloned.1.call-done, bf16[512,7168]{1,0:T(8,128)(2,1)} %get-tuple-element.13), kind=kLoop, calls=%fused_computation.50 | loop fusion | flops 25689600 | bytes 22022144 | tf_op jit(solution)/shard_map/reduce_sum | solution.py:13
  875.9 6.8 fusion.55
  882.8 4.8 fusion.126
  887.6 6.4 convolution_convert_fusion
  897.6 151.5 %all-reduce.11.cloned.1.call-done = bf16[512,7168]{1,0:T(8,128)(2,1)} async-done(((bf16[512,7168]{1,0:T(8,128)(2,1)}), bf16[512,7168]{1,0:T(8,128)(2,1)}) %all-reduce.11.cloned.1.call-update) | async-done | bytes 7340048 | tf_op jit(solution)/shard_map/psum | solution.py:77
  1049.0 10.8 %fusion.41 = bf16[512,7168]{1,0:T(8,128)(2,1)} fusion(bf16[512,7168]{1,0:T(8,128)(2,1)} %get-tuple-element.9, bf16[512,7168]{1,0:T(8,128)(2,1)} %all-reduce.11.cloned.1.call-done), kind=kLoop, calls=%fused_computation.53 | loop fusion | flops 14680064 | bytes 22020096 | tf_op jit(solution)/shard_map/convert_element_type | solution.py:78
  (195 shorter events, 39.7 us)
Async XLA Ops:
  7.2 341.4 %all-reduce.5.cloned.1.call-start = ((), (), s32[]{:S(2)}) async-start(), calls=%async_computation | async-start | bytes 14680064 | tf_op jit(solution)/shard_map/psum | solution.py:74
  7.3 19.6 %copy-start.55 = (f32[32]{0:T(128)}, f32[32]{0:T(128)S(1)}, u32[]{:S(2)}) copy-start(f32[32]{0:T(128)S(1)} %multiply_exponential_fusion) | copy-start | bytes 388
  8.1 18.7 %copy-start.51 = (f32[512]{0:T(512)}, f32[512]{0:T(512)S(1)}, u32[]{:S(2)}) copy-start(f32[512]{0:T(512)S(1)} %convert_element_type.191) | copy-start | bytes 6148
  15.6 8.4 copy-start.16
  15.6 9.8 copy-start.17
  27.1 23.7 %copy-start.24 = (bf16[512,32]{0,1:T(8,128)(2,1)}, bf16[512,32]{0,1:T(8,128)(2,1)S(1)}, u32[]{:S(2)}) copy-start(bf16[512,32]{0,1:T(8,128)(2,1)S(1)} %get-tuple-element.26) | copy-start | bytes 98308
  27.2 23.7 %copy-start.26 = (bf16[512,32]{0,1:T(8,128)(2,1)}, bf16[512,32]{0,1:T(8,128)(2,1)S(1)}, u32[]{:S(2)}) copy-start(bf16[512,32]{0,1:T(8,128)(2,1)S(1)} %get-tuple-element.27) | copy-start | bytes 98308
  27.2 30.1 %copy-start.18 = (f32[512,32]{0,1:T(8,128)}, f32[512,32]{0,1:T(8,128)S(1)}, u32[]{:S(2)}) copy-start(f32[512,32]{0,1:T(8,128)S(1)} %get-tuple-element.36) | copy-start | bytes 196612
  27.2 30.1 %copy-start.20 = (f32[512,32]{0,1:T(8,128)}, f32[512,32]{0,1:T(8,128)S(1)}, u32[]{:S(2)}) copy-start(f32[512,32]{0,1:T(8,128)S(1)} %get-tuple-element.37) | copy-start | bytes 196612
  28.1 22.9 %slice-start = ((s8[4718592]{0:T(1024)(128)(4,1)}), s8[524288]{0:T(1024)(128)(4,1)S(1)}, s32[]{:S(2)}) async-start(s8[4718592]{0:T(1024)(128)(4,1)} %bitcast.152), calls=%async_computation.4 | async-start | bytes 1048576
  31.3 19.7 %slice-start.1 = ((s8[4718592]{0:T(1024)(128)(4,1)}), s8[4194304]{0:T(1024)(128)(4,1)S(1)}, s32[]{:S(2)}) async-start(s8[4718592]{0:T(1024)(128)(4,1)} %bitcast.152), calls=%async_computation.5 | async-start | bytes 8388608
  120.8 16.6 %copy-start.12 = (f32[512,512]{1,0:T(8,128)S(1)}, f32[512,512]{1,0:T(8,128)}, u32[]{:S(2)}) copy-start(f32[512,512]{1,0:T(8,128)} %copy.24) | copy-start | bytes 3145732
  137.4 43.5 %copy-start.23 = (bf16[512,4,128]{2,1,0:T(4,128)(2,1)S(1)}, bf16[512,4,128]{2,1,0:T(4,128)(2,1)}, u32[]{:S(2)}) copy-start(bf16[512,4,128]{2,1,0:T(4,128)(2,1)} %get-tuple-element.29) | copy-start | bytes 1572868
  190.7 342.3 %all-reduce.7.cloned.1.call-start = ((), (), s32[]{:S(2)}) async-start(), calls=%async_computation.1 | async-start | bytes 14680064 | tf_op jit(solution)/shard_map/psum | solution.py:77
  360.2 11.7 %slice-start.2 = ((s8[8257536]{0:T(1024)(128)(4,1)}), s8[4194304]{0:T(1024)(128)(4,1)S(1)}, s32[]{:S(2)}) async-start(s8[8257536]{0:T(1024)(128)(4,1)} %bitcast.182), calls=%async_computation.6 | async-start | bytes 8388608
  378.0 166.6 %copy-start.46 = (f32[1,7168]{1,0:T(1,128)S(1)}, f32[1,7168]{1,0:T(1,128)}, u32[]{:S(2)}) copy-start(f32[1,7168]{1,0:T(1,128)} %get-tuple-element.34) | copy-start | bytes 86020
  378.0 486.2 %all-reduce.9.cloned.1.call-start = ((), (), s32[]{:S(2)}) async-start(), calls=%async_computation.2 | async-start | bytes 14680064 | tf_op jit(solution)/shard_map/psum | solution.py:74
  544.7 9.7 copy-start.52
  544.7 9.7 copy-start.56
  544.7 10.0 copy-start.38
  544.7 10.7 %copy-start.47 = (f32[1,7168]{1,0:T(1,128)S(1)}, f32[1,7168]{1,0:T(1,128)}, u32[]{:S(2)}) copy-start(f32[1,7168]{1,0:T(1,128)} %get-tuple-element.34) | copy-start | bytes 86020
  554.7 20.3 %copy-start.28 = (bf16[512,32]{0,1:T(8,128)(2,1)}, bf16[512,32]{0,1:T(8,128)(2,1)S(1)}, u32[]{:S(2)}) copy-start(bf16[512,32]{0,1:T(8,128)(2,1)S(1)} %get-tuple-element.24) | copy-start | bytes 98308
  554.7 20.3 %copy-start.30 = (bf16[512,32]{0,1:T(8,128)(2,1)}, bf16[512,32]{0,1:T(8,128)(2,1)S(1)}, u32[]{:S(2)}) copy-start(bf16[512,32]{0,1:T(8,128)(2,1)S(1)} %get-tuple-element.25) | copy-start | bytes 98308
  554.7 20.2 %copy-start.44 = (f32[512]{0:T(512)}, f32[512]{0:T(512)S(1)}, u32[]{:S(2)}) copy-start(f32[512]{0:T(512)S(1)} %add_rsqrt_fusion.1) | copy-start | bytes 6148
  555.4 25.3 %copy-start.7 = (bf16[1,1536,4,192]{1,3,2,0:T(8,128)(2,1)S(1)}, bf16[1,1536,4,192]{1,3,2,0:T(8,128)(2,1)}, u32[]{:S(2)}) copy-start(bf16[1,1536,4,192]{1,3,2,0:T(8,128)(2,1)} %get-tuple-element.18) | copy-start | bytes 7077892
  555.4 25.3 %copy-start.53 = (f32[1536]{0:T(1024)S(1)}, f32[1536]{0:T(1024)}, u32[]{:S(2)}) copy-start(f32[1536]{0:T(1024)} %get-tuple-element.6) | copy-start | bytes 18436
  586.7 8.9 copy-start.9
  586.7 8.9 copy-start.15
  655.8 43.5 %copy-start.22 = (bf16[512,4,128]{2,1,0:T(4,128)(2,1)S(1)}, bf16[512,4,128]{2,1,0:T(4,128)(2,1)}, u32[]{:S(2)}) copy-start(bf16[512,4,128]{2,1,0:T(4,128)(2,1)} %get-tuple-element.28) | copy-start | bytes 1572868
  709.2 166.7 %copy-start.48 = (f32[1,7168]{1,0:T(1,128)S(1)}, f32[1,7168]{1,0:T(1,128)}, u32[]{:S(2)}) copy-start(f32[1,7168]{1,0:T(1,128)} %get-tuple-element.32) | copy-start | bytes 86020
  709.2 339.8 %all-reduce.11.cloned.1.call-start = ((), (), s32[]{:S(2)}) async-start(), calls=%async_computation.3 | async-start | bytes 14680064 | tf_op jit(solution)/shard_map/psum | solution.py:77
  875.9 11.6 %slice-start.4 = ((s8[8257536]{0:T(1024)(128)(4,1)}), s8[4194304]{0:T(1024)(128)(4,1)S(1)}, s32[]{:S(2)}) async-start(s8[8257536]{0:T(1024)(128)(4,1)} %bitcast.184), calls=%async_computation.8 | async-start | bytes 8388608
  (36 other events, 173.0 us)
Sparse Core Ops, SparseCore 0:
  190.9 157.6 all-reduce.4
  378.2 154.8 all-reduce.6
  709.3 154.8 all-reduce.8
  894.2 154.7 all-reduce.10
where the time goes:
time: 1070 us
  waiting for transfers between devices  617 us (58%)
  matrix products  333 us (31%)
  other arithmetic  81.5 us (8%)
  local copies, waits for them, and re-layouts  18.8 us (2%)
  between operations  15.2 us (1%)
    psum x2, waiting for transfers between devices, local_layer(): attn_sum = lax.psum(attn_part, 'tp')  311 us
    psum x2, waiting for transfers between devices, local_layer(): mlp_sum = lax.psum(mlp_part, 'tp')  306 us
    dot_general x2, matrix products, latent_attention(): jnp.einsum('bhc,btc->bht', q_lat, ckv_old, preferred_element_type=jnp.flo...  103 us
    dot_general x2, matrix products, latent_attention(): jnp.einsum('bht,btc->bhc', jnp.where(at_pos, bf_zero, attn_prob), ckv_old...  87 us
    reduce_sum x6, other arithmetic, rms_norm(): jnp.mean(values * values, axis=-1, keepdims=True) + NORM_EPS  39.8 us
    dot_general x2, matrix products, attention_heads(): jnp.dot(normed, w_dq, preferred_element_type=jnp.float32)  39.1 us
  transfers between devices with their start and end apart: 4, of which 4 were waited for; matrix products, arithmetic and copies ran while one was open for 0% of the time, Pallas kernels for 0%

commit v1 on v0

v1 whole, which is shorter than its diff:
```python
import functools
import math
import jax
import jax.numpy as jnp
from jax import lax
from jax.experimental import pallas as pl
from jax.experimental.pallas import tpu as pltpu
from jax.sharding import PartitionSpec as P

NORM_EPS = 1e-6
ROPE_BASE = 10000.0
MESH = pl.DeviceIdType.MESH
RING = 8
CHUNK = 32
PIECE = 16
HALF = 256


def rms_norm(values, norm_gain):
    values = values.astype(jnp.float32)
    inv_rms = lax.rsqrt(jnp.mean(values * values, axis=-1, keepdims=True) + NORM_EPS)
    return (values * inv_rms * norm_gain.astype(jnp.float32)).astype(jnp.bfloat16)


def rotary(values, positions):
    half_dim = values.shape[-1] // 2
    inv_freq = jnp.exp(jnp.arange(half_dim, dtype=jnp.float32) * (-2.0 * math.log(ROPE_BASE) / values.shape[-1]))
    angles = positions.astype(jnp.float32)[..., None] * inv_freq
    cos_part = jnp.cos(angles)
    sin_part = jnp.sin(angles)
    lo_half = values[..., :half_dim]
    hi_half = values[..., half_dim:]
    return jnp.concatenate([lo_half * cos_part - hi_half * sin_part, hi_half * cos_part + lo_half * sin_part], axis=-1)


def ring_place():
    index = lax.axis_index('tp')
    core = index % 2
    chip = index // 2
    y = chip % 2
    z = chip // 2
    return core, z * (1 - y) + (7 - z) * y


def ring_device(position, core):
    y = position // 4
    z = position * (1 - y) + (7 - position) * y
    return (z * 2 + y) * 2 + core


def comm_kernel(reduce, norm, gather, canonical, subs, *refs):
    refs = list(refs)
    if reduce:
        part_ref = refs.pop(0)
        hidden_ref = refs.pop(0)
        gain_ref = refs.pop(0) if norm else None
        state_ref = refs.pop(0) if norm else None
        normed_ref = refs.pop(0) if norm and not gather else None
    else:
        shard_ref = refs.pop(0)
    full_ref = refs.pop(0) if gather else None
    if reduce:
        pair_buf, recv_buf, send_buf, pair_send, pair_recv, rs_send, rs_recv = refs[:7]
        refs = refs[7:]
    if gather:
        ag_send, ag_recv, fw_send, fw_recv = refs[:4]
    core, me = ring_place()
    dp_index = lax.axis_index('dp')
    right = (dp_index, ring_device((me + 1) % RING, core))
    left = (dp_index, ring_device((me + RING - 1) % RING, core))
    peer = (dp_index, ring_device(me, 1 - core))
    width = (part_ref if reduce else shard_ref).shape[-1]
    cols = width // subs

    barrier = pltpu.get_barrier_semaphore()
    for other in (left, right, peer):
        pl.semaphore_signal(barrier, inc=1, device_id=other, device_id_type=MESH)
    pl.semaphore_wait(barrier, 3)

    def remote(src, dst, send, recv, target):
        copy = pltpu.make_async_remote_copy(src_ref=src, dst_ref=dst, send_sem=send, recv_sem=recv, device_id=target, device_id_type=MESH)
        copy.start()
        return copy

    pending = []
    ways = ((right, -1), (left, 1))
    if reduce:
        pair_copies = {}
        for step in range(RING):
            for way, (target, sign) in enumerate(ways):
                piece = step * 2 + way
                chunk = (me + RING + sign * (1 + step)) % RING
                row = pl.multiple_of(chunk * CHUNK + way * PIECE, PIECE)
                pair_copies[piece] = remote(part_ref.at[pl.ds(HALF + row, PIECE)], pair_buf.at[piece], pair_send.at[piece], pair_recv.at[piece], peer)
        ring_copies = {}
        for step in range(RING):
            for way, (target, sign) in enumerate(ways):
                piece = step * 2 + way
                chunk = (me + RING + sign * (1 + step)) % RING
                row = pl.multiple_of(chunk * CHUNK + way * PIECE, PIECE)
                pair_copies[piece].wait()
                for sub in range(subs):
                    span = pl.ds(sub * cols, cols)
                    total = part_ref[pl.ds(row, PIECE), span].astype(jnp.float32) + pair_buf[piece, :, span].astype(jnp.float32)
                    if step > 0:
                        before = ring_copies[step - 1, way, sub]
                        before.wait_recv()
                        pending.append(before)
                        total = total + recv_buf[(step - 1) * 2 + way, :, span].astype(jnp.float32)
                    if step < RING - 1:
                        send_buf[piece, :, span] = total.astype(jnp.bfloat16)
                        ring_copies[step, way, sub] = remote(send_buf.at[piece, :, span], recv_buf.at[piece, :, span], rs_send.at[piece * subs + sub], rs_recv.at[piece * subs + sub], target)
                    else:
                        rows = pl.ds(way * PIECE, PIECE)
                        mixed = (hidden_ref[rows, span].astype(jnp.float32) + total).astype(jnp.bfloat16)
                        if norm:
                            state_ref[rows, span] = mixed
                        else:
                            own = pl.multiple_of((core * HALF if canonical else 0) + me * CHUNK + way * PIECE, PIECE)
                            full_ref[pl.ds(own, PIECE), span] = mixed
        if norm:
            for way in range(2):
                rows = pl.ds(way * PIECE, PIECE)
                values = state_ref[rows, :].astype(jnp.float32)
                inv_rms = lax.rsqrt(jnp.mean(values * values, axis=-1, keepdims=True) + NORM_EPS)
                normed = (values * inv_rms * gain_ref[...].astype(jnp.float32)).astype(jnp.bfloat16)
                if gather:
                    own = pl.multiple_of((core * HALF if canonical else 0) + me * CHUNK + way * PIECE, PIECE)
                    full_ref[pl.ds(own, PIECE), :] = normed
                else:
                    normed_ref[rows, :] = normed
    elif gather:
        own = pl.multiple_of((core * HALF if canonical else 0) + me * CHUNK, PIECE)
        full_ref[pl.ds(own, CHUNK), :] = shard_ref[...]
    if gather:
        base_here = core * HALF if canonical else 0
        base_peer = core * HALF if canonical else HALF

        def place(base, chunk, way):
            return pl.ds(pl.multiple_of(base + chunk * CHUNK + way * PIECE, PIECE), PIECE)

        ring_copies = {}
        fw_copies = []
        for step in range(RING):
            for way, (target, sign) in enumerate(ways):
                chunk = (me + RING + sign * step) % RING
                here = place(base_here, chunk, way)
                there = place(base_peer, chunk, way)
                for sub in range(subs):
                    span = pl.ds(sub * cols, cols)
                    slot = (step * 2 + way) * subs + sub
                    if step > 0:
                        before = ring_copies[step - 1, way, sub]
                        before.wait_recv()
                        pending.append(before)
                    if step < RING - 1:
                        ring_copies[step, way, sub] = remote(full_ref.at[here, span], full_ref.at[here, span], ag_send.at[slot], ag_recv.at[slot], target)
                    fw_copies.append(remote(full_ref.at[here, span], full_ref.at[there, span], fw_send.at[slot], fw_recv.at[slot], peer))
        for copy in fw_copies:
            copy.wait()
    for copy in pending:
        copy.wait_send()


def comm_call(call_id, reduce, norm, gather, canonical, subs, operands, width):
    vmem = pl.BlockSpec(memory_space=pltpu.VMEM)
    outs = []
    if reduce and norm:
        outs.append(jax.ShapeDtypeStruct((CHUNK, width), jnp.bfloat16))
        if not gather:
            outs.append(jax.ShapeDtypeStruct((CHUNK, width), jnp.bfloat16))
    if gather:
        outs.append(jax.ShapeDtypeStruct((2 * HALF, width), jnp.bfloat16))
    scratch = []
    dma = pltpu.SemaphoreType.DMA
    if reduce:
        scratch += [pltpu.VMEM((16, PIECE, width), jnp.bfloat16), pltpu.VMEM((14, PIECE, width), jnp.bfloat16), pltpu.VMEM((14, PIECE, width), jnp.bfloat16)]
        scratch += [dma((16,)), dma((16,)), dma((14 * subs,)), dma((14 * subs,))]
    if gather:
        scratch += [dma((14 * subs,)), dma((14 * subs,)), dma((16 * subs,)), dma((16 * subs,))]
    return pl.pallas_call(
        functools.partial(comm_kernel, reduce, norm, gather, canonical, subs),
        out_shape=outs,
        in_specs=[vmem] * len(operands),
        out_specs=[vmem] * len(outs),
        scratch_shapes=scratch,
        compiler_params=pltpu.CompilerParams(collective_id=call_id, has_side_effects=True, vmem_limit_bytes=48 * 1024 * 1024),
        name='comm%d' % call_id,
    )(*operands)


def swap_kernel(src_ref, dst_ref, send_sem, recv_sem):
    core, me = ring_place()
    peer = (lax.axis_index('dp'), ring_device(me, 1 - core))
    barrier = pltpu.get_barrier_semaphore()
    pl.semaphore_signal(barrier, inc=1, device_id=peer, device_id_type=MESH)
    pl.semaphore_wait(barrier, 1)
    copy = pltpu.make_async_remote_copy(src_ref=src_ref, dst_ref=dst_ref, send_sem=send_sem, recv_sem=recv_sem, device_id=peer, device_id_type=MESH)
    copy.start()
    copy.wait()


def swap_call(call_id, block):
    vmem = pl.BlockSpec(memory_space=pltpu.VMEM)
    return pl.pallas_call(
        swap_kernel,
        out_shape=jax.ShapeDtypeStruct(block.shape, block.dtype),
        in_specs=[vmem],
        out_specs=vmem,
        scratch_shapes=[pltpu.SemaphoreType.DMA, pltpu.SemaphoreType.DMA],
        compiler_params=pltpu.CompilerParams(collective_id=call_id, has_side_effects=True),
        name='swap%d' % call_id,
    )(block)


def attention_kernel(block, scale, meta_ref, q_ref, r_ref, ckv_ref, kpe_ref, cnew_ref, knew_ref, out_ref):
    start = meta_ref[0] + pl.program_id(0) * block
    heads, steps = q_ref.shape[1], ckv_ref.shape[2]
    key_steps = lax.broadcasted_iota(jnp.int32, (heads, steps), 1)
    scores = []
    for j in range(block):
        q = q_ref[j]
        r = r_ref[j]
        s = lax.dot_general(q, ckv_ref[0, j], (((1,), (1,)), ((), ())), preferred_element_type=jnp.float32)
        s = s + jnp.dot(r, kpe_ref[0, j], preferred_element_type=jnp.float32)
        scores.append(s)
    probs = []
    fresh_probs = []
    for j in range(block):
        pos = meta_ref[1 + start + j]
        fresh = jnp.sum(q_ref[j].astype(jnp.float32) * cnew_ref[j:j + 1, :].astype(jnp.float32), axis=-1, keepdims=True)
        fresh = fresh + jnp.sum(r_ref[j].astype(jnp.float32) * knew_ref[j:j + 1, :].astype(jnp.float32), axis=-1, keepdims=True)
        at_pos = key_steps == pos
        s = jnp.where(at_pos, fresh, scores[j]) * scale
        s = jnp.where(key_steps <= pos, s, -jnp.inf)
        e = jnp.exp(s - jnp.max(s, axis=-1, keepdims=True))
        p = (e / jnp.sum(e, axis=-1, keepdims=True)).astype(jnp.bfloat16).astype(jnp.float32)
        fresh_probs.append(jnp.sum(jnp.where(at_pos, p, 0.0), axis=-1, keepdims=True))
        probs.append(jnp.where(at_pos, 0.0, p).astype(jnp.bfloat16))
    for j in range(block):
        c = jnp.dot(probs[j], ckv_ref[0, j], preferred_element_type=jnp.float32)
        c = c + fresh_probs[j] * cnew_ref[j:j + 1, :].astype(jnp.float32)
        out_ref[j] = c.astype(jnp.bfloat16)


def attention_call(layer, core, positions, q_lat, q_rope, ckv_cache, kpe_cache, c_new, k_new, scale):
    block = 8
    rows, heads, latent = q_lat.shape
    rope = q_rope.shape[-1]
    steps = ckv_cache.shape[2]
    meta = jnp.concatenate([jnp.reshape(core * HALF, (1,)).astype(jnp.int32), positions])
    blocks = rows // block
    grid_spec = pltpu.PrefetchScalarGridSpec(
        num_scalar_prefetch=1,
        grid=(blocks,),
        in_specs=[
            pl.BlockSpec((block, heads, latent), lambda i, m: (i, 0, 0)),
            pl.BlockSpec((block, heads, rope), lambda i, m: (i, 0, 0)),
            pl.BlockSpec((1, block, steps, latent), lambda i, m: (layer, m[0] // block + i, 0, 0)),
            pl.BlockSpec((1, block, rope, steps), lambda i, m: (layer, m[0] // block + i, 0, 0)),
            pl.BlockSpec((block, latent), lambda i, m: (i, 0)),
            pl.BlockSpec((block, rope), lambda i, m: (i, 0)),
        ],
        out_specs=pl.BlockSpec((block, heads, latent), lambda i, m: (i, 0, 0)),
    )
    return pl.pallas_call(
        functools.partial(attention_kernel, block, scale),
        out_shape=jax.ShapeDtypeStruct((rows, heads, latent), jnp.bfloat16),
        grid_spec=grid_spec,
        compiler_params=pltpu.CompilerParams(vmem_limit_bytes=32 * 1024 * 1024),
        cost_estimate=pl.CostEstimate(flops=4 * rows * heads * steps * latent, bytes_accessed=rows * steps * (latent + rope) * 2, transcendentals=rows * heads * steps),
        name='attention',
    )(meta, q_lat, q_rope, ckv_cache, kpe_cache, c_new, k_new)


def solution(mesh):
    cache_spec = P(None, 'dp', None, None)
    head_spec = P(None, None, 'tp', None)
    weight_specs = (P(), P(), P(), P(), P(), head_spec, head_spec, head_spec, P(None, 'tp', None, None), P(), P(None, None, 'tp'), P(None, None, 'tp'), P(None, 'tp', None))
    in_specs = (P('dp', None), P('dp'), cache_spec, cache_spec) + weight_specs
    out_specs = (P('dp', None), P(None, 'dp', None), P(None, 'dp', None))
    pairs = [(i, i + 1 - 2 * (i % 2)) for i in range(16)]

    def device_body(x_in, pos_ids, ckv_cache, kpe_cache, attn_gain, w_dq, q_gain, w_dkv, kv_gain, w_uq, w_uk, w_uv, w_o, mlp_gain, w_gate, w_up, w_down):
        core, me = ring_place()
        layers, latent = ckv_cache.shape[0], ckv_cache.shape[-1]
        width = x_in.shape[-1]
        nope = w_uk.shape[-1]
        lora = w_dq.shape[-1]
        scale = w_uq.shape[-1] ** -0.5
        first = core * HALF + me * CHUNK
        kpe_t = jnp.swapaxes(kpe_cache, 2, 3)
        p_uq, p_uk, p_uv = [lax.ppermute(w, 'tp', pairs) for w in (w_uq, w_uk, w_uv)]
        state = lax.dynamic_slice_in_dim(x_in, first, CHUNK, 0)
        pos_rows = lax.dynamic_slice_in_dim(pos_ids, first, CHUNK, 0)
        pos_half = lax.dynamic_slice_in_dim(pos_ids, core * HALF, HALF, 0)
        normed = rms_norm(state, attn_gain[0])
        c_rows = []
        k_rows = []
        for layer in range(layers):
            c_q = rms_norm(jnp.dot(normed, w_dq[layer], preferred_element_type=jnp.float32), q_gain[layer])
            kv_lat = jnp.dot(normed, w_dkv[layer], preferred_element_type=jnp.float32)
            c_new = rms_norm(kv_lat[:, :latent], kv_gain[layer])
            k_new = rotary(kv_lat[:, latent:], pos_rows).astype(jnp.bfloat16)
            pad = jnp.zeros((CHUNK, 64), jnp.bfloat16)
            shard = jnp.concatenate([c_q, c_new, k_new, pad], axis=-1)
            latents, = comm_call(1, False, False, True, False, 1, (shard,), shard.shape[-1])
            c_all, k_all = latents[:, lora:lora + latent], latents[:, lora + latent:lora + latent + 64]
            ordered = jnp.where(core == 0, latents[:, lora:lora + latent + 64], jnp.roll(latents[:, lora:lora + latent + 64], HALF, axis=0))
            c_rows.append(ordered[:, :latent])
            k_rows.append(ordered[:, latent:])
            own_q = latents[:HALF, :lora]
            q_lats = []
            q_ropes = []
            for weight_q, weight_k in ((w_uq, w_uk), (p_uq, p_uk)):
                q_full = jnp.einsum('bc,chd->bhd', own_q, weight_q[layer], preferred_element_type=jnp.float32)
                q_nope = q_full[..., :nope].astype(jnp.bfloat16)
                q_ropes.append(rotary(q_full[..., nope:], pos_half[:, None]).astype(jnp.bfloat16))
                q_lats.append(jnp.einsum('bhn,chn->bhc', q_nope, weight_k[layer], preferred_element_type=jnp.float32).astype(jnp.bfloat16))
            q_lat = jnp.concatenate(q_lats, axis=1)
            q_rope = jnp.concatenate(q_ropes, axis=1)
            context = attention_call(layer, core, pos_ids, q_lat, q_rope, ckv_cache, kpe_t, c_all[:HALF], k_all[:HALF], scale)
            heads = w_uv.shape[2]
            own_o = jnp.einsum('bhc,chv->bhv', context[:, :heads], w_uv[layer], preferred_element_type=jnp.float32).astype(jnp.bfloat16)
            peer_o = jnp.einsum('bhc,chv->bhv', context[:, heads:], p_uv[layer], preferred_element_type=jnp.float32).astype(jnp.bfloat16)
            peer_o = swap_call(2, peer_o.reshape(HALF, -1))
            head_out = jnp.concatenate([own_o.reshape(HALF, -1), peer_o], axis=0)
            attn_part = jnp.dot(head_out, w_o[layer].reshape(-1, width), preferred_element_type=jnp.float32).astype(jnp.bfloat16)
            state, mlp_in = comm_call(3, True, True, True, False, 2, (attn_part, state, mlp_gain[layer][None]), width)
            gate_pre = jnp.dot(mlp_in, w_gate[layer], preferred_element_type=jnp.float32)
            up_pre = jnp.dot(mlp_in, w_up[layer], preferred_element_type=jnp.float32)
            act_out = (jax.nn.silu(gate_pre) * up_pre).astype(jnp.bfloat16)
            mlp_part = jnp.dot(act_out, w_down[layer], preferred_element_type=jnp.float32).astype(jnp.bfloat16)
            if layer + 1 < layers:
                state, normed = comm_call(4, True, True, False, False, 2, (mlp_part, state, attn_gain[layer + 1][None]), width)
            else:
                x_out, = comm_call(5, True, False, True, True, 2, (mlp_part, state), width)
        return x_out, jnp.stack(c_rows), jnp.stack(k_rows)

    return jax.shard_map(device_body, mesh=mesh, in_specs=in_specs, out_specs=out_specs, check_vma=False)
```

time: 1070 us -> 661 us (0.62)
  waiting for transfers between devices: 617 us -> 0.01 us
  Pallas kernels: 0 us -> 462 us
  matrix products: 333 us -> 113 us
  other arithmetic: 81.5 us -> 12.5 us
  local copies, waits for them, and re-layouts: 18.8 us -> 62.2 us
  between operations: 15.2 us -> 1.9 us
    psum x4 -> x0, waiting for transfers between devices: 617 us -> none  [the longest x2 311 us: local_layer(): attn_sum = lax.psum(attn_part, 'tp')]
    pallas_call x0 -> x10, Pallas kernels: none -> 462 us  [the longest x6 365 us: comm_call(): pl.pallas_call(functools.partial(comm_kernel, reduce, norm, gather, canon...]
    dot_general x24 -> x20, matrix products: 328 us -> 106 us  [the longest x2 20.6 us: device_body(): jnp.dot(head_out, w_o[layer].reshape(-1, width), preferred_element_type=j...]
    reduce_sum x6 -> x3, other arithmetic: 39.8 us -> 1.61 us  [rms_norm(): jnp.mean(values * values, axis=-1, keepdims=True) + NORM_EPS]
    unnamed x129 -> x88, local copies, waits for them, and re-layouts: 4.64 us -> 30.1 us
    slice x2 -> x16, local copies, waits for them, and re-layouts: 3.03 us -> 25.6 us  [the longest x1 10.6 us: device_body(): w_o[layer].reshape(-1, width)]
    reduce_sum x2 -> x0, other arithmetic: 14.8 us -> none  [latent_attention(): jnp.sum(jnp.where(at_pos, attn_prob, bf_zero), axis=-1).astype(jnp.float32)]
    convert_element_type x3 -> x0, other arithmetic: 10.9 us -> none  [the longest x1 10.8 us: local_layer(): (mid_state.astype(jnp.float32) + mlp_sum.astype(jnp.float32)).astype(jnp....]
  transfers between devices with their start and end apart: 4 -> 3, of which waited for: 4 -> 0; matrix products, arithmetic and copies ran while one was open for 0% -> 10% of each run, Pallas kernels for 0% -> 12%
where the time goes in v1:
time: 661 us; the launch traced here: 653 us
  Pallas kernels  462 us (70%)
  matrix products  113 us (17%)
  local copies, waits for them, and re-layouts  62.2 us (9%)
  other arithmetic  12.5 us (2%)
    pallas_call x6, Pallas kernels, comm_call(): pl.pallas_call(functools.partial(comm_kernel, reduce, norm, gather, canon...  365 us
    pallas_call x2, Pallas kernels, attention_call(): pl.pallas_call(functools.partial(attention_kernel, block, scale), out_sha...  91.1 us
    unnamed x88, local copies, waits for them, and re-layouts  30.1 us
    dot_general x2, matrix products, device_body(): jnp.dot(head_out, w_o[layer].reshape(-1, width), preferred_element_type=j...  20.6 us
    dot_general x2, matrix products, device_body(): jnp.dot(normed, w_dq[layer], preferred_element_type=jnp.float32)  18.9 us
    dot_general x2, matrix products, device_body(): up_pre = jnp.dot(mlp_in, w_up[layer], preferred_element_type=jnp.float32)  18.6 us
  transfers between devices with their start and end apart: 3, of which 0 were waited for; matrix products, arithmetic and copies ran while one was open for 10% of the time, Pallas kernels for 12%

profile of v1, /device:TPU:0, one launch (start us, length us, event | category | flops | bytes accessed | tf_op | source)
XLA Modules:
  0.0 652.6 jit_solution(8544436398160555896)
XLA Ops:
  6.4 4.9 fusion.82
  13.4 9.6 %multiply_reduce_fusion.1 = (f32[32]{0:T(128)S(1)}, f32[32,1536]{1,0:T(8,128)S(1)}) fusion(bf16[2,7168,1536]{2,1,0:T(8,128)(2,1)} %param.22, bf16[32,7168]{1,0:T(8,128)(2,1)S(1)} %get-tuple-element.21.refs_1_, f32[7168]{0:T(1024)S(1)} %bitcast.155, f32[32]{0:T(128)S(1)} %add_rsqrt_fusion.4), kind=kOutput, calls=%fused_computation.104 | convolution fusion | flops 705658880 | bytes 22704384 | tf_op jit(solution)/shard_map/dot_general | solution.py:301
  24.2 2.5 fusion.8
  27.4 30.1 %comm1.2 = bf16[512,2176]{1,0:T(8,128)(2,1)S(1)} custom-call(bf16[32,2176]{1,0:T(8,128)(2,1)S(1)} %concatenate.58.refs_0_), custom_call_target="tpu_custom_call" | custom-call | tf_op jit(solution)/shard_map/comm1/pallas_call | solution.py:181
  57.5 2.5 fusion.53
  61.0 2.5 convolution_convert_fusion.7
  63.5 3.1 copy.84
  71.8 10.6 %fusion.81 = (bf16[1,4,128,7168]{3,2,1,0:T(8,128)(2,1)}, bf16[1,4,128,7168]{3,2,1,0:T(8,128)(2,1)}) fusion(bf16[2,4,128,7168]{3,2,1,0:T(8,128)(2,1)} %param.29), kind=kLoop, calls=%fused_computation.148 | loop fusion | bytes 29360128 | tf_op jit(solution)/shard_map/slice | solution.py:328
  82.4 4.3 fusion.83
  99.7 45.6 %attention.2 = bf16[256,8,512]{2,1,0:T(8,128)(2,1)S(1)} custom-call(s32[513]{0:T(1024)S(1)} %pad_add_fusion.meta_ref, bf16[256,8,512]{2,1,0:T(8,128)(2,1)S(1)} %pad_maximum_fusion.q_ref, bf16[256,8,64]{2,1,0:T(8,128)(2,1)S(1)} %maximum_maximum_fusion.r_ref, bf16[2,512,256,512]{3,2,1,0:T(8,128)(2,1)} %ckv_ref.3, bf16[2,512,64,256]{3,2,1,0:T(8,128)(2,1)} %bitcast.133, ...), custom_call_target="tpu_custom_call" | custom-call | flops 1073741824 | bytes 75497472 | tf_op jit(solution)/shard_map/attention/pallas_call | solution.py:266
  149.4 3.2 swap2.2
  152.6 2.6 convolution_convert_fusion.11
  156.3 10.2 %convolution_convert_fusion.3.refs_0_ = bf16[512,7168]{1,0:T(8,128)(2,1)} fusion(bf16[512,7168]{1,0:T(8,128)(2,1)} %bitcast.136, bf16[256,512]{1,0:T(8,128)(2,1)} %swap2.2, bf16[256,512]{1,0:T(8,128)(2,1)S(1)} %copy.55), kind=kOutput, calls=%fused_computation.9 | convolution fusion | flops 3762814976 | bytes 15204352 | tf_op jit(solution)/shard_map/dot_general | solution.py:328
  166.5 87.8 %comm3.2 = (bf16[32,7168]{1,0:T(8,128)(2,1)S(1)}, bf16[512,7168]{1,0:T(8,128)(2,1)}) custom-call(bf16[512,7168]{1,0:T(8,128)(2,1)} %convolution_convert_fusion.3.refs_0_, bf16[32,7168]{1,0:T(8,128)(2,1)S(1)} %get-tuple-element.21.refs_1_, bf16[1,7168]{1,0:T(2,128)(2,1)S(1)} %get-tuple-element.61.refs_2_), custom_call_target="tpu_custom_call" | custom-call | tf_op jit(solution)/shard_map/comm3/pallas_call | solution.py:181
  254.4 6.7 %fusion.20 = f32[512,288]{0,1:T(8,128)S(1)} fusion(bf16[512,7168]{1,0:T(8,128)(2,1)} %get-tuple-element.9, bf16[2,7168,288]{1,2,0:T(8,128)(2,1)} %param.31), kind=kOutput, calls=%fused_computation.24 | convolution fusion | flops 2113929216 | bytes 12058624 | tf_op jit(solution)/shard_map/dot_general | solution.py:330
  261.9 13.6 %fusion.37 = bf16[512,288]{0,1:T(8,128)(2,1)S(1)} fusion(bf16[512,7168]{1,0:T(8,128)(2,1)S(1)} %copy-done.23, bf16[2,7168,288]{1,2,0:T(8,128)(2,1)S(1)} %bitcast.164, f32[512,288]{0,1:T(8,128)S(1)} %fusion.20), kind=kOutput, calls=%fused_computation.41 | convolution fusion | flops 2114813952 | bytes 12353536 | tf_op jit(solution)/shard_map/dot_general | solution.py:331
  275.6 6.1 convolution_convert_fusion.2.refs_0_
  281.6 44.7 %comm4.1 = (bf16[32,7168]{1,0:T(8,128)(2,1)S(1)}, bf16[32,7168]{1,0:T(8,128)(2,1)S(1)}) custom-call(bf16[512,7168]{1,0:T(8,128)(2,1)} %convolution_convert_fusion.2.refs_0_, bf16[32,7168]{1,0:T(8,128)(2,1)S(1)} %get-tuple-element.10.refs_1_, bf16[1,7168]{1,0:T(2,128)(2,1)S(1)} %get-tuple-element.62.refs_2_), custom_call_target="tpu_custom_call" | custom-call | tf_op jit(solution)/shard_map/comm4/pallas_call | solution.py:181
  326.3 9.3 %multiply_reduce_fusion = (f32[32]{0:T(128)S(1)}, f32[32,1536]{1,0:T(8,128)S(1)}) fusion(bf16[32,7168]{1,0:T(8,128)(2,1)S(1)} %get-tuple-element.11, bf16[2,7168,1536]{2,1,0:T(8,128)(2,1)} %param.22), kind=kOutput, calls=%fused_computation.102 | convolution fusion | flops 704741376 | bytes 22675584 | tf_op jit(solution)/shard_map/dot_general | solution.py:301
  335.7 5.8 fusion.6
  342.1 26.5 %comm1.3 = bf16[512,2176]{1,0:T(8,128)(2,1)S(1)} custom-call(bf16[32,2176]{1,0:T(8,128)(2,1)S(1)} %concatenate.64.refs_0_), custom_call_target="tpu_custom_call" | custom-call | tf_op jit(solution)/shard_map/comm1/pallas_call | solution.py:181
  368.6 2.5 fusion.49
  371.1 2.5 convolution_convert_fusion.5
  387.5 45.5 %attention.3 = bf16[256,8,512]{2,1,0:T(8,128)(2,1)S(1)} custom-call(s32[513]{0:T(1024)S(1)} %pad_add_fusion.meta_ref, bf16[256,8,512]{2,1,0:T(8,128)(2,1)S(1)} %pad_maximum_fusion.1.q_ref, bf16[256,8,64]{2,1,0:T(8,128)(2,1)S(1)} %maximum_maximum_fusion.1.r_ref, bf16[2,512,256,512]{3,2,1,0:T(8,128)(2,1)} %ckv_ref.3, bf16[2,512,64,256]{3,2,1,0:T(8,128)(2,1)} %bitcast.134, ...), custom_call_target="tpu_custom_call" | custom-call | flops 1073741824 | bytes 75497472 | tf_op jit(solution)/shard_map/attention/pallas_call | solution.py:266
  436.1 3.2 swap2.3
  441.0 10.4 %convolution_convert_fusion.1.refs_0_ = bf16[512,7168]{1,0:T(8,128)(2,1)} fusion(bf16[512,7168]{1,0:T(8,128)(2,1)} %bitcast.135, bf16[256,512]{1,0:T(8,128)(2,1)} %swap2.3, bf16[256,512]{1,0:T(8,128)(2,1)S(1)} %copy.57), kind=kOutput, calls=%fused_computation.7 | convolution fusion | flops 3762814976 | bytes 15204352 | tf_op jit(solution)/shard_map/dot_general | solution.py:328
  451.4 88.0 %comm3.3 = (bf16[32,7168]{1,0:T(8,128)(2,1)S(1)}, bf16[512,7168]{1,0:T(8,128)(2,1)}) custom-call(bf16[512,7168]{1,0:T(8,128)(2,1)} %convolution_convert_fusion.1.refs_0_, bf16[32,7168]{1,0:T(8,128)(2,1)S(1)} %get-tuple-element.12.refs_1_, bf16[1,7168]{1,0:T(2,128)(2,1)S(1)} %get-tuple-element.60.refs_2_), custom_call_target="tpu_custom_call" | custom-call | tf_op jit(solution)/shard_map/comm3/pallas_call | solution.py:181
  539.5 5.6 fusion.15
  545.1 5.0 fusion.34
  550.1 6.1 convolution_convert_fusion.refs_0_
  556.2 87.4 %comm5.1 = bf16[512,7168]{1,0:T(8,128)(2,1)} custom-call(bf16[512,7168]{1,0:T(8,128)(2,1)} %convolution_convert_fusion.refs_0_, bf16[32,7168]{1,0:T(8,128)(2,1)S(1)} %get-tuple-element.14.refs_1_), custom_call_target="tpu_custom_call" | custom-call | tf_op jit(solution)/shard_map/comm5/pallas_call | solution.py:181
  645.5 6.6 %copy.86 = bf16[512,7168]{1,0:T(8,128)(2,1)} copy(bf16[512,7168]{1,0:T(8,128)(2,1)} %comm5.1) | data formatting | bytes 14680064
  (160 shorter events, 55.7 us)
Async XLA Ops:
  3.0 85.3 %collective-permute-start.1 = (bf16[2,512,4,128]{3,1,2,0:T(8,128)(2,1)}, bf16[2,512,4,128]{3,1,2,0:T(8,128)(2,1)}, u32[]{:S(2)}, u32[]{:S(2)}) collective-permute-start(bf16[2,512,4,128]{3,1,2,0:T(8,128)(2,1)} %copy.20), channel_id=1, source_target_pairs={{0,1},{1,0},{2,3},{3,2},{4,5},{5,4},{6,7},{7,6},{8,9},{9,8},{10,11... | collective-permute-start | bytes 3145736 | tf_op jit(solution)/shard_map/ppermute | solution.py:293
  3.5 78.9 %collective-permute-start = (bf16[2,1536,4,192]{1,3,2,0:T(8,128)(2,1)}, bf16[2,1536,4,192]{1,3,2,0:T(8,128)(2,1)}, u32[]{:S(2)}, u32[]{:S(2)}) collective-permute-start(bf16[2,1536,4,192]{1,3,2,0:T(8,128)(2,1)} %param.26), channel_id=1, source_target_pairs={{0,1},{1,0},{2,3},{3,2},{4,5},{5,4},{6,7},{7,6},{8,9},{9,8},{10,11... | collective-permute-start | bytes 14155784 | tf_op jit(solution)/shard_map/ppermute | solution.py:293
  5.9 141.2 %collective-permute-start.2 = (bf16[2,512,4,128]{1,3,2,0:T(8,128)(2,1)}, bf16[2,512,4,128]{1,3,2,0:T(8,128)(2,1)}, u32[]{:S(2)}, u32[]{:S(2)}) collective-permute-start(bf16[2,512,4,128]{1,3,2,0:T(8,128)(2,1)} %copy.30), channel_id=1, source_target_pairs={{0,1},{1,0},{2,3},{3,2},{4,5},{5,4},{6,7},{7,6},{8,9},{9,8},{10,11... | collective-permute-start | bytes 3145736 | tf_op jit(solution)/shard_map/ppermute | solution.py:293
  6.4 4.9 copy-start.17
  6.4 6.3 copy-start.20
  11.3 11.6 %slice-start = ((s8[16515072]{0:T(1024)(128)(4,1)}), s8[4194304]{0:T(1024)(128)(4,1)S(1)}, s32[]{:S(2)}) async-start(s8[16515072]{0:T(1024)(128)(4,1)} %bitcast.159), calls=%async_computation | async-start | bytes 8388608
  13.4 9.6 %slice-start.1 = ((s8[16515072]{0:T(1024)(128)(4,1)}), s8[4194304]{0:T(1024)(128)(4,1)S(1)}, s32[]{:S(2)}) async-start(s8[16515072]{0:T(1024)(128)(4,1)} %bitcast.159), calls=%async_computation.1 | async-start | bytes 8388608
  13.4 9.7 %slice-start.2 = ((s8[16515072]{0:T(1024)(128)(4,1)}), s8[4194304]{0:T(1024)(128)(4,1)S(1)}, s32[]{:S(2)}) async-start(s8[16515072]{0:T(1024)(128)(4,1)} %bitcast.159), calls=%async_computation.2 | async-start | bytes 8388608
  13.4 10.8 %slice-start.3 = ((s8[16515072]{0:T(1024)(128)(4,1)}), s8[3932160]{0:T(1024)(128)(4,1)S(1)}, s32[]{:S(2)}) async-start(s8[16515072]{0:T(1024)(128)(4,1)} %bitcast.159), calls=%async_computation.3 | async-start | bytes 7864320
  60.0 11.7 %copy-start.18 = (bf16[2,7168]{1,0:T(2,128)(2,1)S(1)}, bf16[2,7168]{1,0:T(2,128)(2,1)}, u32[]{:S(2)}) copy-start(bf16[2,7168]{1,0:T(2,128)(2,1)} %param.30) | copy-start | bytes 86020
  95.5 3.2 copy-start
  95.5 3.2 copy-start.2
  166.5 94.6 %slice-start.6 = ((s8[8257536]{0:T(1024)(128)(4,1)}), s8[4194304]{0:T(1024)(128)(4,1)S(1)}, s32[]{:S(2)}) async-start(s8[8257536]{0:T(1024)(128)(4,1)} %bitcast.163), calls=%async_computation.6 | async-start | bytes 8388608
  254.3 6.8 %slice-start.7 = ((s8[8257536]{0:T(1024)(128)(4,1)}), s8[4063232]{0:T(1024)(128)(4,1)S(1)}, s32[]{:S(2)}) async-start(s8[8257536]{0:T(1024)(128)(4,1)} %bitcast.163), calls=%async_computation.7 | async-start | bytes 8126464
  254.3 7.6 %copy-start.23 = (bf16[512,7168]{1,0:T(8,128)(2,1)S(1)}, bf16[512,7168]{1,0:T(8,128)(2,1)}, u32[]{:S(2)}) copy-start(bf16[512,7168]{1,0:T(8,128)(2,1)} %get-tuple-element.9) | copy-start | bytes 22020100
  254.3 21.2 %slice-start.8 = ((s8[8257536]{0:T(1024)(128)(4,1)}), s8[4194304]{0:T(1024)(128)(4,1)S(1)}, s32[]{:S(2)}) async-start(s8[8257536]{0:T(1024)(128)(4,1)} %bitcast.165), calls=%async_computation.8 | async-start | bytes 8388608
  261.9 13.6 %slice-start.9 = ((s8[8257536]{0:T(1024)(128)(4,1)}), s8[4063232]{0:T(1024)(128)(4,1)S(1)}, s32[]{:S(2)}) async-start(s8[8257536]{0:T(1024)(128)(4,1)} %bitcast.165), calls=%async_computation.9 | async-start | bytes 8126464
  335.7 6.2 copy-start.19
  368.6 5.8 copy-start.10
  373.6 3.0 copy-start.3
  374.8 3.7 copy-start.15
  376.6 6.6 %copy-start.1 = (bf16[4,256,512]{2,1,0:T(8,128)(2,1)S(1)}, bf16[4,256,512]{2,1,0:T(8,128)(2,1)}, u32[]{:S(2)}) copy-start(bf16[4,256,512]{2,1,0:T(8,128)(2,1)} %convolution_convert_fusion.5) | copy-start | bytes 3145732
  377.4 3.1 copy-start.13
  383.3 2.8 copy-start.4
  383.3 2.8 copy-start.5
  441.0 98.5 %slice-start.4 = ((s8[8257536]{0:T(1024)(128)(4,1)}), s8[4194304]{0:T(1024)(128)(4,1)S(1)}, s32[]{:S(2)}) async-start(s8[8257536]{0:T(1024)(128)(4,1)} %bitcast.161), calls=%async_computation.4 | async-start | bytes 8388608
  441.0 98.5 %slice-start.5 = ((s8[8257536]{0:T(1024)(128)(4,1)}), s8[4063232]{0:T(1024)(128)(4,1)S(1)}, s32[]{:S(2)}) async-start(s8[8257536]{0:T(1024)(128)(4,1)} %bitcast.161), calls=%async_computation.5 | async-start | bytes 8126464
  539.5 5.6 copy-start.24
  539.5 10.6 %slice-start.10 = ((s8[8257536]{0:T(1024)(128)(4,1)}), s8[4194304]{0:T(1024)(128)(4,1)S(1)}, s32[]{:S(2)}) async-start(s8[8257536]{0:T(1024)(128)(4,1)} %bitcast.167), calls=%async_computation.10 | async-start | bytes 8388608
  545.1 5.0 slice-start.11
  556.2 88.3 %copy-start.8 = (bf16[1,512,512]{2,1,0:T(8,128)(2,1)S(1)}, bf16[1,512,512]{2,1,0:T(8,128)(2,1)}, u32[]{:S(2)}) copy-start(bf16[1,512,512]{2,1,0:T(8,128)(2,1)} %slice_bitcast_fusion) | copy-start | bytes 1572868
  556.2 88.3 %copy-start.9 = (bf16[1,512,512]{2,1,0:T(8,128)(2,1)S(1)}, bf16[1,512,512]{2,1,0:T(8,128)(2,1)}, u32[]{:S(2)}) copy-start(bf16[1,512,512]{2,1,0:T(8,128)(2,1)} %slice_bitcast_fusion.1) | copy-start | bytes 1572868
  (8 other events, 19.9 us)
